TPU v7x, 256 devices: a whole 4x4x8 slice. The times are simulated.
256 devices in a mesh: band: 128 (over z, y, x), ch: 2 (over core).
Axes of the slice: x: 4, y: 4, z: 8, core: 2. Of those that a mesh axis runs over, the one named last changes fastest.
Arguments:
- grid_field: bfloat16 [100, 2097152], P(None, 'band'), may hold values from -6 to 6
- band_points: int32 [128], P('band'), may hold values from 8192 to 16384
- block_ids: int32 [128, 16], P('band'), may hold values from 0 to 4095, as said below
- block_count: int32 [128], P('band'), may hold values from 8 to 16
- block_weight: bfloat16 [128, 16, 256, 512], P('band'), may hold values from 0 to 0.039794922
- embed_weight: bfloat16 [100, 1024], P(None, 'ch'), may hold values from -0.3125 to 0.3125
- edge_src: int32 [655360], P('band'), may hold values from 0 to 32767, as said below
- edge_dst: int32 [655360], P('band'), may hold values from 0 to 32767, as said below
- edge_in_weight: bfloat16 [2, 1024, 1024], P(None, None, 'ch'), may hold values from -0.1875 to 0.1875
- edge_out_weight: bfloat16 [1024, 1024], P('ch'), may hold values from -0.0625 to 0.0625
- node_in_weight: bfloat16 [2, 1024, 1024], P(None, None, 'ch'), may hold values from -0.125 to 0.125
- node_out_weight: bfloat16 [1024, 1024], P('ch'), may hold values from -0.1875 to 0.1875
Outputs:
- node_state: bfloat16 [32768, 1024], P('band', 'ch')
Inputs may be any that keep to these rules, and one draw needn't show every extreme that they name: For band b, block_ids[b, k] * 512 lies from max(b * 16384 - 16384 // 2, 0) to min((b + 1) * 16384 + 16384 // 2, 2097152) - 512; both ends are named by every band; ids may repeat. `edge_src`: edge e belongs to band b = e // 5120; its source node lies in bands b - 1 to b + 1 of the mesh. `edge_dst`: edge e ends at a node of its band b = e // 5120.
All inputs are finite; a program needn't handle non-finite values.
Results may differ from a plain program's by a relative error of at most 0.015.
Values may be sent and summed in bfloat16 or wider, within the bound.
A program may use at most 64 MiB of HBM per device.

v0:
```python
import jax
import jax.numpy as jnp
from jax import lax
from jax.sharding import PartitionSpec as P


def extended_2(block, sides, width):
    for axis, dim in sides:
        count = lax.axis_size(axis)
        forward = [(i, i + 1) for i in range(count - 1)]
        backward = [(target, source) for source, target in forward]
        low = lax.ppermute(
            lax.slice_in_dim(block, block.shape[dim] - width, None, axis=dim), axis, forward
        )
        high = lax.ppermute(lax.slice_in_dim(block, 0, width, axis=dim), axis, backward)
        block = jnp.concatenate([low, block, high], axis=dim)
    return block


def sent_to_all(x, axis):
    copies = jnp.broadcast_to(x, (lax.axis_size(axis), *x.shape))
    return lax.all_to_all(copies, axis, split_axis=0, concat_axis=0, tiled=True)


def in_order(blocks, dim):
    lengths = list(blocks.shape[1:])
    lengths[dim] *= blocks.shape[0]
    return jnp.moveaxis(blocks, 0, dim).reshape(lengths)


def gather_directly(x, axis, dim):
    blocks = sent_to_all(x, axis)
    return in_order(blocks, dim)


def split_up(x, dim, size):
    before, after = (x.shape[:dim], x.shape[dim + 1 :])
    return jnp.moveaxis(x.reshape(*before, size, -1, *after), dim, 0)


def summed_on_arrival(x, axis, dim):
    blocks = split_up(x, dim, lax.axis_size(axis))
    arrived = lax.all_to_all(blocks, axis, split_axis=0, concat_axis=0, tiled=True)
    return arrived.astype(jnp.float32).sum(axis=0)


def on_device(
    grid_field,
    band_points,
    block_ids,
    block_count,
    block_weight,
    embed_weight,
    edge_src,
    edge_dst,
    edge_in_weight,
    edge_out_weight,
    node_in_weight,
    node_out_weight,
):
    band_index = lax.axis_index("band")
    channels, points = grid_field.shape
    kblocks = block_weight.shape[1]
    node_count = block_weight.shape[2]
    block_len = block_weight.shape[3]
    sub_count = points // block_len
    column = lax.broadcasted_iota(jnp.int32, (1, points), 1)
    live = jnp.where(column < band_points[0], grid_field, jnp.zeros_like(grid_field))
    share = channels // lax.axis_size("ch")
    local_live = lax.dynamic_slice_in_dim(live, lax.axis_index("ch") * share, share, 0)
    extended = extended_2(local_live, (("band", 1),), points // 2)
    first_block = band_index * sub_count - sub_count // 2
    ext_blocks = extended.shape[1] // block_len
    tiles = extended.reshape(extended.shape[0], ext_blocks, block_len)
    local_ids = block_ids[0] - first_block
    tile_ids = lax.broadcasted_iota(jnp.int32, (kblocks, ext_blocks), 1)
    slot_live = lax.broadcasted_iota(jnp.int32, (kblocks, ext_blocks), 0) < block_count[0]
    selector = ((local_ids[:, None] == tile_ids) & slot_live).astype(jnp.bfloat16)
    blocks = jnp.einsum("ks,csp->kcp", selector, tiles, preferred_element_type=jnp.float32).astype(
        jnp.bfloat16
    )
    remapped = jnp.einsum(
        "knp,kcp->nc", block_weight[0], blocks, preferred_element_type=jnp.float32
    ).astype(jnp.bfloat16)
    remapped = gather_directly(remapped, "ch", 1)
    initial = jnp.dot(remapped, embed_weight, preferred_element_type=jnp.float32).astype(
        jnp.bfloat16
    )
    shard_part = lax.all_gather(initial, "ch", axis=1, tiled=True)
    rows_src = edge_in_weight[0]
    rows_dst = edge_in_weight[1]
    rows_node = node_in_weight[0]
    source_acc = jnp.dot(shard_part, rows_src, preferred_element_type=jnp.float32)
    target_acc = jnp.dot(shard_part, rows_dst, preferred_element_type=jnp.float32)
    direct = jnp.dot(shard_part, rows_node, preferred_element_type=jnp.float32)
    source_proj = source_acc.astype(jnp.bfloat16)
    target_proj = target_acc.astype(jnp.bfloat16)
    source_ext = extended_2(source_proj, (("band", 0),), node_count)
    src_local = edge_src - (band_index - 1) * node_count
    dst_local = edge_dst - band_index * node_count
    pre_act = jnp.take(source_ext, src_local, axis=0).astype(jnp.float32) + jnp.take(
        target_proj, dst_local, axis=0
    ).astype(jnp.float32)
    edge_hidden = jax.nn.silu(pre_act).astype(jnp.bfloat16)
    messages = jnp.dot(edge_hidden, edge_out_weight, preferred_element_type=jnp.float32)
    node_ids = lax.broadcasted_iota(jnp.int32, (node_count, 1), 0)
    onehot = (dst_local[None, :] == node_ids).astype(jnp.float32)
    partial_agg = jnp.dot(onehot, messages, preferred_element_type=jnp.float32)
    agg_half = summed_on_arrival(partial_agg.astype(jnp.bfloat16), "ch", 1).astype(jnp.bfloat16)
    rows_agg = node_in_weight[1]
    from_agg = jnp.dot(
        gather_directly(agg_half, "ch", 1), rows_agg, preferred_element_type=jnp.float32
    )
    update = jax.nn.silu(direct + from_agg).astype(jnp.bfloat16)
    partial_out = jnp.dot(update, node_out_weight, preferred_element_type=jnp.float32)
    summed = summed_on_arrival(partial_out.astype(jnp.bfloat16), "ch", 1)
    return (initial.astype(jnp.float32) + summed).astype(jnp.bfloat16)


def solution(mesh):
    return jax.shard_map(
        on_device,
        mesh=mesh,
        in_specs=(
            P(None, "band"),
            P("band"),
            P("band", None),
            P("band"),
            P("band", None, None, None),
            P(None, "ch"),
            P("band"),
            P("band"),
            P(None, None, "ch"),
            P("ch", None),
            P(None, None, "ch"),
            P("ch", None),
        ),
        out_specs=P("band", "ch"),
        check_vma=False,
    )
```

profile of v0, /device:TPU:127, one launch (start us, length us, event | category | flops | bytes accessed | tf_op | source)
XLA Modules:
  0.0 141.0 jit_solution(9254778661560007322)
XLA Ops:
  0.0 0.0 copy-start
  0.0 0.0 copy-start.6
  0.0 0.0 copy-start.3
  0.0 0.0 copy-start.4
  0.8 2.1 %dynamic-slice_select_fusion = bf16[50,16384]{1,0:T(8,128)(2,1)S(1)} fusion(bf16[100,16384]{1,0:T(8,128)(2,1)} %param.12, s32[]{:T(128)S(6)} %select_n.25, pred[16384]{0:T(1024)(128)(4,1)S(1)} %iota_compare_fusion.4), kind=kLoop, calls=%fused_computation.18 | loop fusion | flops 819200 | bytes 3293188 | tf_op jit(solution)/shard_map/jit(_where)/select_n | solution.py:68
  2.9 1.4 fusion.62
  4.2 4.3 %collective-permute-start = (bf16[50,8192]{1,0:T(8,128)(2,1)}, bf16[50,8192]{1,0:T(8,128)(2,1)}, u32[]{:S(2)}, u32[]{:S(2)}) collective-permute-start(bf16[50,8192]{1,0:T(8,128)(2,1)} %get-tuple-element.7), channel_id=1, source_target_pairs={{0,2},{2,4},{4,6},{6,8},{8,10},{10,12},{12,14},{14,16},{16,18},{18... | collective-permute-start | bytes 2457608 | tf_op jit(solution)/shard_map/ppermute | solution.py:12
  8.6 1.9 %collective-permute-start.1 = (bf16[50,8192]{1,0:T(8,128)(2,1)}, bf16[50,8192]{1,0:T(8,128)(2,1)}, u32[]{:S(2)}, u32[]{:S(2)}) collective-permute-start(bf16[50,8192]{1,0:T(8,128)(2,1)} %get-tuple-element.8), channel_id=1, source_target_pairs={{2,0},{4,2},{6,4},{8,6},{10,8},{12,10},{14,12},{16,14},{18,16},{20... | collective-permute-start | bytes 2457608 | tf_op jit(solution)/shard_map/ppermute | solution.py:15
  10.5 0.0 copy-done.6
  11.2 0.0 copy-done.3
  11.2 0.0 copy-done.4
  11.3 16.5 %collective-permute-done = bf16[50,8192]{1,0:T(8,128)(2,1)} collective-permute-done((bf16[50,8192]{1,0:T(8,128)(2,1)}, bf16[50,8192]{1,0:T(8,128)(2,1)}, u32[]{:S(2)}, u32[]{:S(2)}) %collective-permute-start) | collective-permute-done | bytes 819232 | tf_op jit(solution)/shard_map/ppermute | solution.py:12
  27.8 9.3 %collective-permute-done.1 = bf16[50,8192]{1,0:T(8,128)(2,1)} collective-permute-done((bf16[50,8192]{1,0:T(8,128)(2,1)}, bf16[50,8192]{1,0:T(8,128)(2,1)}, u32[]{:S(2)}, u32[]{:S(2)}) %collective-permute-start.1) | collective-permute-done | bytes 819232 | tf_op jit(solution)/shard_map/ppermute | solution.py:15
  37.1 1.7 %pad_maximum_fusion = bf16[50,32768]{1,0:T(8,128)(2,1)S(1)} fusion(bf16[50,8192]{1,0:T(8,128)(2,1)} %collective-permute-done.1, bf16[50,16384]{1,0:T(8,128)(2,1)S(1)} %dynamic-slice_select_fusion, bf16[50,8192]{1,0:T(8,128)(2,1)} %collective-permute-done), kind=kLoop, calls=%fused_computation.13 | loop fusion | flops 9830400 | bytes 6553600 | tf_op jit(solution)/shard_map/concatenate | solution.py:16
  38.8 0.0 copy-start.1
  38.8 1.4 copy.22
  40.2 0.0 copy-start.2
  40.2 0.6 fusion.20
  40.8 0.2 copy-done.1
  41.0 1.6 %fusion.32 = bf16[256,50]{0,1:T(8,128)(2,1)S(1)} fusion(bf16[1,16,256,512]{3,2,1,0:T(8,128)(2,1)S(1)} %copy-done.1, bf16[16,50,512]{2,0,1:T(8,128)(2,1)S(1)} %fusion.20), kind=kOutput, calls=%fused_computation.28 | convolution fusion | flops 209728000 | bytes 5039104 | tf_op jit(solution)/shard_map/knp,kcp->nc/dot_general | solution.py:82
  42.6 5.3 %all_to_all.20 = bf16[2,256,50]{1,2,0:T(8,128)(2,1)S(1)} all-to-all(bf16[2,256,50]{1,2,0:T(8,128)(2,1)S(1)} %broadcast_in_dim.43), channel_id=1, replica_groups=mesh['band'=128,'ch'=2] {'ch'}, dimensions={0} | all-to-all | bytes 102400 | tf_op jit(solution)/shard_map/all_to_all | solution.py:22
  47.9 0.0 copy-done.2
  47.9 0.2 convolution_convert_fusion.3
  48.2 2.2 %all_gather.3 = bf16[256,1024]{1,0:T(8,128)(2,1)S(1)} all-gather(bf16[256,512]{1,0:T(8,128)(2,1)S(1)} %convolution_convert_fusion.3), channel_id=1, replica_groups=mesh['band'=128,'ch'=2] {'ch'}, dimensions={1}, use_global_device_ids=true | all-gather | bytes 786432 | tf_op jit(solution)/shard_map/all_gather | solution.py:89
  50.4 1.7 %convolution_convert_fusion.2 = bf16[256,512]{1,0:T(8,128)(2,1)S(1)} fusion(bf16[256,1024]{1,0:T(8,128)(2,1)S(1)} %all_gather.3, bf16[2,1024,512]{2,1,0:T(8,128)(2,1)} %param.20), kind=kOutput, calls=%fused_computation.24 | convolution fusion | flops 268566528 | bytes 1835008 | tf_op jit(solution)/shard_map/dot_general | solution.py:93
  52.0 1.7 %convolution_convert_fusion.1 = bf16[256,512]{1,0:T(8,128)(2,1)S(1)} fusion(bf16[256,1024]{1,0:T(8,128)(2,1)S(1)} %all_gather.3, bf16[2,1024,512]{2,1,0:T(8,128)(2,1)} %param.20), kind=kOutput, calls=%fused_computation.23 | convolution fusion | flops 268566528 | bytes 1835008 | tf_op jit(solution)/shard_map/dot_general | solution.py:94
  53.7 1.9 %collective-permute-start.3 = (bf16[256,512]{1,0:T(8,128)(2,1)S(1)}, bf16[256,512]{1,0:T(8,128)(2,1)S(1)}, u32[]{:S(2)}, u32[]{:S(2)}) collective-permute-start(bf16[256,512]{1,0:T(8,128)(2,1)S(1)} %convolution_convert_fusion.2), channel_id=1, source_target_pairs={{2,0},{4,2},{6,4},{8,6},{10,8},{12,10},{14,12},{16,14},{18,16},{20... | collective-permute-start | bytes 786440 | tf_op jit(solution)/shard_map/ppermute | solution.py:15
  55.6 9.0 %collective-permute-start.2 = (bf16[256,512]{1,0:T(8,128)(2,1)S(1)}, bf16[256,512]{1,0:T(8,128)(2,1)S(1)}, u32[]{:S(2)}, u32[]{:S(2)}) collective-permute-start(bf16[256,512]{1,0:T(8,128)(2,1)S(1)} %convolution_convert_fusion.2), channel_id=1, source_target_pairs={{0,2},{2,4},{4,6},{6,8},{8,10},{10,12},{12,14},{14,16},{16,18},{18... | collective-permute-start | bytes 786440 | tf_op jit(solution)/shard_map/ppermute | solution.py:12
  64.6 21.4 %gather_fusion.1 = bf16[5120,512]{1,0:T(8,128)(2,1)} fusion(bf16[256,512]{1,0:T(8,128)(2,1)S(1)} %convolution_convert_fusion.1, s32[5120]{0:T(1024)S(1)} %fusion.50), kind=kCustom, calls=%fused_computation.1 | custom fusion | bytes 10506240 | tf_op jit(solution)/shard_map/jit(_take)/gather | solution.py:101
  86.0 2.5 %fusion.38 = f32[256,512]{1,0:T(8,128)} fusion(bf16[256,1024]{1,0:T(8,128)(2,1)S(1)} %all_gather.3, bf16[2,1024,512]{2,1,0:T(8,128)(2,1)} %param.22), kind=kOutput, calls=%fused_computation.32 | convolution fusion | flops 268435456 | bytes 2097152 | tf_op jit(solution)/shard_map/dot_general | solution.py:95
  88.5 0.0 collective-permute-done.3
  88.5 0.0 collective-permute-done.2
  88.5 0.1 pad_maximum_fusion.1
  88.5 21.4 %gather_fusion = bf16[5120,512]{1,0:T(8,128)(2,1)} fusion(bf16[768,512]{1,0:T(8,128)(2,1)S(1)} %pad_maximum_fusion.1, s32[5120]{0:T(1024)S(1)} %fusion.51), kind=kCustom, calls=%fused_computation | custom fusion | bytes 10506240 | tf_op jit(solution)/shard_map/jit(_take)/gather | solution.py:101
  109.9 0.0 copy-done
  109.9 14.5 %fusion.23 = bf16[256,1024]{1,0:T(8,128)(2,1)S(1)} fusion(bf16[512,1024]{1,0:T(8,128)(2,1)S(1)} %copy-done, bf16[5120,512]{1,0:T(8,128)(2,1)} %gather_fusion.1, bf16[5120,512]{1,0:T(8,128)(2,1)} %gather_fusion, pred[5120]{0:T(1024)(128)(4,1)S(1)} %get-tuple-element.5, pred[5120]{0:T(1024)(128)(4,1)S(1)} %get-tuple-element.9, s32[5120]{0:T(1024)S(1)} %get-tuple-element.6), kind=kOutput, calls=%fused_computation.21 | convolution fusion | flops 8080850944 | bytes 12089344 | tf_op jit(solution)/shard_map/dot_general | solution.py:108
  124.4 0.0 copy-start.5
  124.4 4.8 %all_to_all.21 = bf16[2,256,512]{2,1,0:T(8,128)(2,1)S(1)} all-to-all(bf16[2,256,512]{2,1,0:T(8,128)(2,1)S(1)} %bitcast.75), channel_id=1, replica_groups=mesh['band'=128,'ch'=2] {'ch'}, dimensions={0} | all-to-all | bytes 1048576 | tf_op jit(solution)/shard_map/all_to_all | solution.py:43
  129.2 0.1 reduce_sum.21
  129.3 0.1 copy.17
  129.5 4.2 %all_to_all.22 = bf16[2,256,512]{1,2,0:T(8,128)(2,1)S(1)} all-to-all(bf16[2,256,512]{1,2,0:T(8,128)(2,1)S(1)} %broadcast_in_dim.49), channel_id=1, replica_groups=mesh['band'=128,'ch'=2] {'ch'}, dimensions={0} | all-to-all | bytes 1048576 | tf_op jit(solution)/shard_map/all_to_all | solution.py:22
  133.7 0.0 copy-done.5
  133.7 2.3 %convolution_convert_fusion = bf16[256,1024]{1,0:T(8,128)(2,1)S(1)} fusion(bf16[512,1024]{1,0:T(8,128)(2,1)S(1)} %copy-done.5, f32[256,512]{1,0:T(8,128)} %fusion.38, bf16[256,1024]{0,1:T(8,128)(2,1)S(1)} %bitcast.78, bf16[2,1024,512]{2,1,0:T(8,128)(2,1)} %param.22), kind=kOutput, calls=%fused_computation.20 | convolution fusion | flops 537919488 | bytes 3670016 | tf_op jit(solution)/shard_map/dot_general | solution.py:115
  136.0 4.2 %all_to_all.23 = bf16[2,256,512]{2,1,0:T(8,128)(2,1)S(1)} all-to-all(bf16[2,256,512]{2,1,0:T(8,128)(2,1)S(1)} %bitcast.76), channel_id=1, replica_groups=mesh['band'=128,'ch'=2] {'ch'}, dimensions={0} | all-to-all | bytes 1048576 | tf_op jit(solution)/shard_map/all_to_all | solution.py:43
  140.1 0.1 convert_reduce_fusion
  140.2 0.8 add_convert_fusion
  (11 shorter events, 0.2 us)
Async XLA Ops:
  0.0 109.9 %copy-start = (bf16[512,1024]{1,0:T(8,128)(2,1)S(1)}, bf16[512,1024]{1,0:T(8,128)(2,1)}, u32[]{:S(2)}) copy-start(bf16[512,1024]{1,0:T(8,128)(2,1)} %param.21) | copy-start | bytes 3145732
  0.0 10.5 %copy-start.6 = (s32[1,16]{1,0:T(1,128)S(1)}, s32[1,16]{1,0:T(1,128)}, u32[]{:S(2)}) copy-start(s32[1,16]{1,0:T(1,128)} %param.14) | copy-start | bytes 196
  0.0 11.2 %copy-start.3 = (s32[5120]{0:T(1024)S(1)}, s32[5120]{0:T(1024)}, u32[]{:S(2)}) copy-start(s32[5120]{0:T(1024)} %param.18) | copy-start | bytes 61444
  0.0 11.2 %copy-start.4 = (s32[5120]{0:T(1024)S(1)}, s32[5120]{0:T(1024)}, u32[]{:S(2)}) copy-start(s32[5120]{0:T(1024)} %param.19) | copy-start | bytes 61444
  4.2 23.6 %collective-permute-start = (bf16[50,8192]{1,0:T(8,128)(2,1)}, bf16[50,8192]{1,0:T(8,128)(2,1)}, u32[]{:S(2)}, u32[]{:S(2)}) collective-permute-start(bf16[50,8192]{1,0:T(8,128)(2,1)} %get-tuple-element.7), channel_id=1, source_target_pairs={{0,2},{2,4},{4,6},{6,8},{8,10},{10,12},{12,14},{14,16},{16,18},{18... | collective-permute-start | bytes 2457608 | tf_op jit(solution)/shard_map/ppermute | solution.py:12
  8.6 28.5 %collective-permute-start.1 = (bf16[50,8192]{1,0:T(8,128)(2,1)}, bf16[50,8192]{1,0:T(8,128)(2,1)}, u32[]{:S(2)}, u32[]{:S(2)}) collective-permute-start(bf16[50,8192]{1,0:T(8,128)(2,1)} %get-tuple-element.8), channel_id=1, source_target_pairs={{2,0},{4,2},{6,4},{8,6},{10,8},{12,10},{14,12},{16,14},{18,16},{20... | collective-permute-start | bytes 2457608 | tf_op jit(solution)/shard_map/ppermute | solution.py:15
  38.8 2.2 %copy-start.1 = (bf16[1,16,256,512]{3,2,1,0:T(8,128)(2,1)S(1)}, bf16[1,16,256,512]{3,2,1,0:T(8,128)(2,1)}, u32[]{:S(2)}) copy-start(bf16[1,16,256,512]{3,2,1,0:T(8,128)(2,1)} %param.16) | copy-start | bytes 12582916
  40.2 7.7 %copy-start.2 = (bf16[100,512]{1,0:T(8,128)(2,1)S(1)}, bf16[100,512]{1,0:T(8,128)(2,1)}, u32[]{:S(2)}) copy-start(bf16[100,512]{1,0:T(8,128)(2,1)} %param.17) | copy-start | bytes 307204
  53.7 34.8 %collective-permute-start.3 = (bf16[256,512]{1,0:T(8,128)(2,1)S(1)}, bf16[256,512]{1,0:T(8,128)(2,1)S(1)}, u32[]{:S(2)}, u32[]{:S(2)}) collective-permute-start(bf16[256,512]{1,0:T(8,128)(2,1)S(1)} %convolution_convert_fusion.2), channel_id=1, source_target_pairs={{2,0},{4,2},{6,4},{8,6},{10,8},{12,10},{14,12},{16,14},{18,16},{20... | collective-permute-start | bytes 786440 | tf_op jit(solution)/shard_map/ppermute | solution.py:15
  55.6 32.8 %collective-permute-start.2 = (bf16[256,512]{1,0:T(8,128)(2,1)S(1)}, bf16[256,512]{1,0:T(8,128)(2,1)S(1)}, u32[]{:S(2)}, u32[]{:S(2)}) collective-permute-start(bf16[256,512]{1,0:T(8,128)(2,1)S(1)} %convolution_convert_fusion.2), channel_id=1, source_target_pairs={{0,2},{2,4},{4,6},{6,8},{8,10},{10,12},{12,14},{14,16},{16,18},{18... | collective-permute-start | bytes 786440 | tf_op jit(solution)/shard_map/ppermute | solution.py:12
  124.4 9.3 %copy-start.5 = (bf16[512,1024]{1,0:T(8,128)(2,1)S(1)}, bf16[512,1024]{1,0:T(8,128)(2,1)}, u32[]{:S(2)}) copy-start(bf16[512,1024]{1,0:T(8,128)(2,1)} %param.23) | copy-start | bytes 3145732
where the time goes:
time: 142 us; the launch traced here: 141 us
  local copies, waits for them, and re-layouts  46 us (32%)
  waiting for transfers between devices  25.8 us (18%)
  matrix products  24.9 us (18%)
  blocking collectives  20.6 us (15%)
  starting transfers between devices  17.1 us (12%)
  other arithmetic  4.87 us (3%)
  between operations  1.67 us (1%)
    gather x1, local copies, waits for them, and re-layouts, on_device(): jnp.take(target_proj, dst_local, axis=0).astype(jnp.float32)  21.4 us
    gather x1, local copies, waits for them, and re-layouts, on_device(): jnp.take(source_ext, src_local, axis=0).astype(jnp.float32)  21.4 us
    ppermute x2, waiting for transfers between devices, extended_2(): lax.ppermute(lax.slice_in_dim(block, block.shape[dim] - width, None, axis...  16.5 us
    dot_general x1, matrix products, on_device(): partial_agg = jnp.dot(onehot, messages, preferred_element_type=jnp.float32)  14.5 us
    ppermute x2, starting transfers between devices, extended_2(): lax.ppermute(lax.slice_in_dim(block, block.shape[dim] - width, None, axis...  13.3 us
    all_to_all x2, blocking collectives, sent_to_all(): return lax.all_to_all(copies, axis, split_axis=0, concat_axis=0, tiled=True)  9.49 us
    ppermute x2, waiting for transfers between devices, extended_2(): lax.ppermute(lax.slice_in_dim(block, 0, width, axis=dim), axis, backward)  9.27 us
    all_to_all x2, blocking collectives, summed_on_arrival(): lax.all_to_all(blocks, axis, split_axis=0, concat_axis=0, tiled=True)  8.97 us
  transfers between devices with their start and end apart: 4, of which 2 were waited for; matrix products, arithmetic and copies ran while one was open for 17% of the time, Pallas kernels for 0%

commit v1 on v0

v1 whole, which is shorter than its diff:
```python
import jax
import jax.numpy as jnp
from jax import lax
from jax.experimental import pallas as pl
from jax.experimental.pallas import tpu as pltpu
from jax.sharding import PartitionSpec as P

MESH = pl.DeviceIdType.MESH
F32 = jnp.float32
BF16 = jnp.bfloat16
NN = (((1,), (0,)), ((), ()))
NT = (((1,), (1,)), ((), ()))
LANES = 128


def mm(a, b, dims=NN):
    return lax.dot_general(a, b, dims, preferred_element_type=F32)


def build(n_band, cin, points, kblocks, node, blk, hidden, edges):
    half = hidden // 2
    hb = blk // 2
    sub = points // blk
    side = sub // 2
    ext = 2 * sub
    chunks = edges // LANES
    step_e = 512
    steps = edges // step_e

    def kernel(
        ids, cnt, bp, src, dst, field, bw, emb, ein, eout, nin, nout, out,
        X, XS, W, E, EP, WI, WN, WO, NO, EW, EN, M, OS, OD, ODT, HB, BPV, BPL,
        PO, PP, RX, G, DIR, INI, SB, UB,
        s_right, r_right, s_left, r_left, s_x, r_x, s_r, r_r, loc, l_own, l_w,
    ):
        b = lax.axis_index("band")
        c = lax.axis_index("ch")
        right = lax.rem(b + 1, n_band)
        left = lax.rem(b + n_band - 1, n_band)
        me_p = (b, 1 - c)
        to_right = (right, c)
        to_left = (left, c)
        col = pl.multiple_of(c * hb, hb)

        bar = pltpu.get_barrier_semaphore()
        for dev in (me_p, to_right, to_left):
            pl.semaphore_signal(bar, inc=1, device_id=dev, device_id_type=MESH)
        pl.semaphore_wait(bar, 3)

        def remote(s, d, ss, rs, dev):
            return pltpu.make_async_remote_copy(
                src_ref=s, dst_ref=d, send_sem=ss, recv_sem=rs, device_id=dev, device_id_type=MESH
            )

        halo = []
        for j in range(side):
            lo = pl.ds(pl.multiple_of(j * blk + col, LANES), hb)
            hi = pl.ds(pl.multiple_of((side + j) * blk + col, LANES), hb)
            halo.append(remote(field.at[:, hi], X.at[j], s_right.at[j], r_right.at[j], to_right))
            halo.append(remote(field.at[:, lo], X.at[side + sub + j], s_left.at[j], r_left.at[j], to_left))
        for d in halo:
            d.start()

        BPV[...] = jnp.full(BPV.shape, bp[0], jnp.int32)

        oc = pl.multiple_of((1 - c) * half, half)
        mc = pl.multiple_of(c * half, half)
        swaps = [
            remote(emb, E.at[c], s_x.at[0], r_x.at[0], me_p),
            remote(eout, WO.at[c], s_x.at[1], r_x.at[1], me_p),
            remote(nout.at[:, pl.ds(oc, half)], NO.at[c], s_x.at[2], r_x.at[2], me_p),
        ]
        for d in swaps:
            d.start()
        locs = [
            pltpu.make_async_copy(emb, E.at[c], loc.at[0]),
            pltpu.make_async_copy(ein, WI, loc.at[1]),
            pltpu.make_async_copy(nin, WN, loc.at[2]),
            pltpu.make_async_copy(eout, WO.at[c], loc.at[3]),
            pltpu.make_async_copy(nout.at[:, pl.ds(mc, half)], NO.at[c], loc.at[4]),
        ]
        for d in locs:
            d.start()
        own = []
        for j in range(sub):
            own.append(pltpu.make_async_copy(
                field.at[:, pl.ds(pl.multiple_of(j * blk + col, LANES), hb)], X.at[side + j], l_own.at[j]))
        for k in range(kblocks):
            own.append(pltpu.make_async_copy(
                bw.at[0, k, :, pl.ds(col, hb)], W.at[:, pl.ds(k * hb, hb)], l_w.at[k]))
        for d in own:
            d.start()

        live_bp = remote(BPV, BPL, s_x.at[3], r_x.at[3], to_right)

        eye_r = lax.broadcasted_iota(jnp.int32, (LANES, LANES), 0)
        eye_c = lax.broadcasted_iota(jnp.int32, (LANES, LANES), 1)
        eye = jnp.where(eye_r == eye_c, 1.0, 0.0)
        eye2 = jnp.concatenate([eye, eye * 256.0], axis=1).astype(BF16)
        eye1 = eye.astype(BF16)
        lane_i = lax.broadcasted_iota(jnp.int32, (LANES, LANES), 1).astype(F32)
        sub_i = lax.broadcasted_iota(jnp.int32, (node, LANES), 0)
        src0 = (b - 1) * node
        dst0 = b * node

        @pl.loop(0, chunks)
        def _(j):
            s = src[pl.ds(j, 1), :] - src0
            d = dst[pl.ds(j, 1), :] - dst0
            s_lo = jnp.broadcast_to((s & 255).astype(F32), (LANES, LANES))
            s_hi = jnp.broadcast_to((s >> 8).astype(F32), (LANES, LANES))
            d_f = jnp.broadcast_to(d.astype(F32), (LANES, LANES))
            s_cols = mm(eye2, jnp.concatenate([s_lo, s_hi], axis=1).astype(BF16), NT)
            d_cols = mm(eye1, d_f.astype(BF16), NT)
            rows = pl.ds(pl.multiple_of(j * LANES, LANES), LANES)
            for t in range(3 * node // LANES):
                OS[rows, t * LANES:(t + 1) * LANES] = jnp.where(
                    s_cols == lane_i + float(t * LANES), 1.0, 0.0).astype(BF16)
            for t in range(node // LANES):
                OD[rows, t * LANES:(t + 1) * LANES] = jnp.where(
                    d_cols == lane_i + float(t * LANES), 1.0, 0.0).astype(BF16)
            ODT[:, rows] = jnp.where(jnp.broadcast_to(d, (node, LANES)) == sub_i, 1.0, 0.0).astype(BF16)

        live_bp.start()
        XS[...] = jnp.zeros(XS.shape, BF16)
        EP[...] = jnp.zeros(EP.shape, BF16)

        for d in locs:
            d.wait()
        for d in swaps:
            d.wait()
        for q in range(2):
            EP[q, 0:cin, :] = E[q]
        for a in range(2):
            EW[a * LANES:(a + 1) * LANES, :] = (0.5 * (
                mm(EP[0], WI[a, 0:half, :]) + mm(EP[1], WI[a, half:hidden, :]))).astype(BF16)
        EN[...] = (mm(EP[0], WN[0, 0:half, :]) + mm(EP[1], WN[0, half:hidden, :])).astype(BF16)

        @pl.loop(0, 2 * half // LANES)
        def _(t):
            q = t // (half // LANES)
            rows = pl.ds(pl.multiple_of((t % (half // LANES)) * LANES, LANES), LANES)
            M[q, rows, :] = mm(WO[q, rows, :], WN[1]).astype(BF16)

        for d in own:
            d.wait()
        live_bp.wait()
        for d in halo:
            d.wait()

        first = b * sub - side
        lane = lax.broadcasted_iota(jnp.int32, (cin, hb), 1)
        big = jnp.int32(2 * points)
        for k in range(kblocks):
            i = jnp.clip(ids[0, k] - first, 0, ext - 1)
            x = X[i]
            base = jnp.where(i < side, i + side, i - side) * blk + col
            lim = jnp.where(i < side, BPL[0:1, :], jnp.where(i < side + sub, bp[0], big))
            lim = jnp.where(k < cnt[0], lim, 0)
            x = jnp.where(lane + base < lim, x, jnp.zeros_like(x))
            XS[0:cin, k * hb:(k + 1) * hb] = x
        PO[...] = mm(W[...], XS[...], NT)
        part = remote(PO, PP, s_x.at[4], r_x.at[4], me_p)
        part.start()
        part.wait()
        RX[1] = (PO[...] + PP[...]).astype(BF16)
        spread = [
            remote(RX.at[1], RX.at[0], s_r.at[0], r_r.at[0], to_right),
            remote(RX.at[1], RX.at[2], s_r.at[1], r_r.at[1], to_left),
        ]
        for d in spread:
            d.start()
        INI[...] = mm(RX[1], EP[c]).astype(BF16)
        DIR[...] = mm(RX[1], EN[...])
        for d in spread:
            d.wait()

        for t in range(steps):
            rows = slice(t * step_e, (t + 1) * step_e)
            gs = mm(OS[rows, 0:node], RX[0]) + mm(OS[rows, node:2 * node], RX[1]) + mm(OS[rows, 2 * node:3 * node], RX[2])
            gd = mm(OD[rows, :], RX[1])
            g = jnp.concatenate([gs, gd], axis=1).astype(BF16)
            u = mm(g, EW[...])
            HB[rows, :] = (u + u * jnp.tanh(u)).astype(BF16)
        SB[c] = mm(ODT[...], HB[...]).astype(BF16)
        sx = remote(SB.at[c], SB.at[c], s_x.at[5], r_x.at[5], me_p)
        sx.start()
        DIR[...] = DIR[...] + mm(SB[c], M[c])
        sx.wait()
        v = 0.5 * (DIR[...] + mm(SB[1 - c], M[1 - c]))
        UB[c] = (v + v * jnp.tanh(v)).astype(BF16)
        ux = remote(UB.at[c], UB.at[c], s_x.at[6], r_x.at[6], me_p)
        ux.start()
        acc = INI[...].astype(F32) + mm(UB[c], NO[c])
        ux.wait()
        out[...] = (acc + mm(UB[1 - c], NO[1 - c])).astype(BF16)

    V = pltpu.VMEM
    D = pltpu.SemaphoreType.DMA
    scratch = [
        V((ext, cin, hb), BF16),
        V((LANES, kblocks * hb), BF16),
        V((node, kblocks * hb), BF16),
        V((2, cin, half), BF16),
        V((2, LANES, half), BF16),
        V((2, hidden, half), BF16),
        V((2, hidden, half), BF16),
        V((2, half, hidden), BF16),
        V((2, half, half), BF16),
        V((2 * LANES, half), BF16),
        V((LANES, half), BF16),
        V((2, half, half), BF16),
        V((edges, 3 * node), BF16),
        V((edges, node), BF16),
        V((node, edges), BF16),
        V((edges, half), BF16),
        V((8, hb), jnp.int32),
        V((8, hb), jnp.int32),
        V((node, LANES), F32),
        V((node, LANES), F32),
        V((3, node, LANES), BF16),
        V((8, LANES), BF16),
        V((node, half), F32),
        V((node, half), BF16),
        V((2, node, half), BF16),
        V((2, node, half), BF16),
        D((side,)), D((side,)), D((side,)), D((side,)),
        D((7,)), D((7,)), D((2,)), D((2,)), D((5,)), D((sub,)), D((kblocks,)),
    ]
    smem = pl.BlockSpec(memory_space=pltpu.SMEM)
    vmem = pl.BlockSpec(memory_space=pltpu.VMEM)
    hbm = pl.BlockSpec(memory_space=pl.ANY)
    return pl.pallas_call(
        kernel,
        out_shape=jax.ShapeDtypeStruct((node, half), BF16),
        in_specs=[smem, smem, smem, vmem, vmem] + [hbm] * 7,
        out_specs=vmem,
        scratch_shapes=scratch,
        compiler_params=pltpu.CompilerParams(
            collective_id=0, has_side_effects=True, vmem_limit_bytes=63 * 1024 * 1024
        ),
        name="remap_layer",
    )


def solution(mesh):
    n_band = mesh.shape["band"]

    def on_device(grid_field, band_points, block_ids, block_count, block_weight, embed_weight,
                  edge_src, edge_dst, edge_in_weight, edge_out_weight, node_in_weight, node_out_weight):
        cin, points = grid_field.shape
        _, kblocks, node, blk = block_weight.shape
        hidden = edge_in_weight.shape[1]
        edges = edge_src.shape[0]
        call = build(n_band, cin, points, kblocks, node, blk, hidden, edges)
        return call(
            block_ids, block_count, band_points,
            edge_src.reshape(-1, LANES), edge_dst.reshape(-1, LANES),
            grid_field, block_weight, embed_weight, edge_in_weight,
            edge_out_weight, node_in_weight, node_out_weight,
        )

    return jax.shard_map(
        on_device,
        mesh=mesh,
        in_specs=(
            P(None, "band"), P("band"), P("band", None), P("band"), P("band", None, None, None),
            P(None, "ch"), P("band"), P("band"), P(None, None, "ch"), P("ch", None),
            P(None, None, "ch"), P("ch", None),
        ),
        out_specs=P("band", "ch"),
        check_vma=False,
    )
```

time: 142 us -> 58.3 us (0.41)
  the two profiles are of different devices: /device:TPU:127 before, /device:TPU:1 now
where the time goes in v1:
time: 58.3 us; the launch traced here: 58.2 us
  Pallas kernels  55.2 us (95%)
  local copies, waits for them, and re-layouts  1.67 us (3%)
  between operations  1.3 us (2%)
    pallas_call x1, Pallas kernels, on_device(): call(block_ids, block_count, band_points, edge_src.reshape(-1, LANES), ed...  55.2 us
    unnamed x1, local copies, waits for them, and re-layouts  1.67 us

profile of v1, /device:TPU:1, one launch (start us, length us, event | category | flops | bytes accessed | tf_op | source)
XLA Modules:
  0.0 58.2 jit_solution(12014852165022333124)
XLA Ops:
  1.3 55.2 %remap_layer.1 = bf16[256,512]{1,0:T(8,128)(2,1)} custom-call(s32[1,16]{1,0:T(1,128)} %ids.1, s32[1]{0:T(128)S(6)} %copy.15.cnt, s32[1]{0:T(128)S(6)} %copy.14.bp, s32[40,128]{1,0:T(8,128)} %bitcast.2, s32[40,128]{1,0:T(8,128)} %bitcast.3, bf16[100,16384]{1,0:T(8,128)(2,1)} %field.1, bf16[1,16,256,512]{3,2,1,0:T(8,128)(2,1)} %bw.1, bf16[100,512]{1,0:T(8,128)(2,1)} %emb.1, ...), custom_call_target="tpu_custom_call" | custom-call | tf_op jit(solution)/shard_map/remap_layer/pallas_call | solution.py:256
  56.5 1.7 %copy.16 = bf16[256,512]{1,0:T(8,128)(2,1)} copy(bf16[256,512]{1,0:T(8,128)(2,1)} %remap_layer.1) | data formatting | bytes 524288

commit v2 on v1

--- a/solution.py
+++ b/solution.py
@@ -28,11 +28,17 @@
     steps = edges // step_e
 
     def kernel(
-        ids, cnt, bp, src, dst, field, bw, emb, ein, eout, nin, nout, out,
-        X, XS, W, E, EP, WI, WN, WO, NO, EW, EN, M, OS, OD, ODT, HB, BPV, BPL,
-        PO, PP, RX, G, DIR, INI, SB, UB,
-        s_right, r_right, s_left, r_left, s_x, r_x, s_r, r_r, loc, l_own, l_w,
+        cnt, bp, ids_h, src_h, dst_h, field, bw, emb, ein, eout, nin, nout, out,
+        ids, src, dst, X, XS, W, E, EP, WI, WN, WO, NO, EW, EN, M, OS, OD, ODT, MK, HB, BPV, BPL,
+        PO, PP, RO, RN, GO, DIR, INI, SB, UB,
+        s_right, r_right, s_left, r_left, s_x, r_x, s_r, r_r, loc, l_own, l_w, l_in,
     ):
+        inputs = [
+            pltpu.make_async_copy(h, v, l_in.at[n])
+            for n, (h, v) in enumerate(((src_h, src), (dst_h, dst), (ids_h, ids)))
+        ]
+        for d in inputs:
+            d.start()
         b = lax.axis_index("band")
         c = lax.axis_index("ch")
         right = lax.rem(b + 1, n_band)
@@ -42,27 +48,60 @@
         to_left = (left, c)
         col = pl.multiple_of(c * hb, hb)
 
+        has_right = b < n_band - 1
+        has_left = b > 0
+
         bar = pltpu.get_barrier_semaphore()
-        for dev in (me_p, to_right, to_left):
+
+        def greet(dev):
             pl.semaphore_signal(bar, inc=1, device_id=dev, device_id_type=MESH)
-        pl.semaphore_wait(bar, 3)
+
+        greet(me_p)
+        pl.when(has_right)(lambda: greet(to_right))
+        pl.when(has_left)(lambda: greet(to_left))
+        neighbours = (b + n_band - 1) // n_band + (2 * n_band - 2 - b) // n_band
+        pl.semaphore_wait(bar, 1 + neighbours)
+
+        def begin(to_r, to_l):
+            @pl.when(has_right)
+            def _():
+                for d in to_r:
+                    d.start()
+
+            @pl.when(has_left)
+            def _():
+                for d in to_l:
+                    d.start()
+
+        def finish(to_r, to_l):
+            @pl.when(has_right)
+            def _():
+                for d in to_r:
+                    d.wait_send()
+                for d in to_l:
+                    d.wait_recv()
+
+            @pl.when(has_left)
+            def _():
+                for d in to_l:
+                    d.wait_send()
+                for d in to_r:
+                    d.wait_recv()
 
         def remote(s, d, ss, rs, dev):
             return pltpu.make_async_remote_copy(
                 src_ref=s, dst_ref=d, send_sem=ss, recv_sem=rs, device_id=dev, device_id_type=MESH
             )
 
-        halo = []
+        halo_r, halo_l = [], []
         for j in range(side):
             lo = pl.ds(pl.multiple_of(j * blk + col, LANES), hb)
             hi = pl.ds(pl.multiple_of((side + j) * blk + col, LANES), hb)
-            halo.append(remote(field.at[:, hi], X.at[j], s_right.at[j], r_right.at[j], to_right))
-            halo.append(remote(field.at[:, lo], X.at[side + sub + j], s_left.at[j], r_left.at[j], to_left))
-        for d in halo:
-            d.start()
+            halo_r.append(remote(field.at[:, hi], X.at[j], s_right.at[j], r_right.at[j], to_right))
+            halo_l.append(remote(field.at[:, lo], X.at[side + sub + j], s_left.at[j], r_left.at[j], to_left))
+        begin(halo_r, halo_l)
 
         BPV[...] = jnp.full(BPV.shape, bp[0], jnp.int32)
-
         oc = pl.multiple_of((1 - c) * half, half)
         mc = pl.multiple_of(c * half, half)
         swaps = [
@@ -93,12 +132,12 @@
 
         live_bp = remote(BPV, BPL, s_x.at[3], r_x.at[3], to_right)
 
+        for d in inputs:
+            d.wait()
         eye_r = lax.broadcasted_iota(jnp.int32, (LANES, LANES), 0)
         eye_c = lax.broadcasted_iota(jnp.int32, (LANES, LANES), 1)
-        eye = jnp.where(eye_r == eye_c, 1.0, 0.0)
-        eye2 = jnp.concatenate([eye, eye * 256.0], axis=1).astype(BF16)
-        eye1 = eye.astype(BF16)
-        lane_i = lax.broadcasted_iota(jnp.int32, (LANES, LANES), 1).astype(F32)
+        eye = jnp.where(eye_r == eye_c, 1.0, 0.0).astype(BF16)
+        lane_i = eye_c.astype(F32)
         sub_i = lax.broadcasted_iota(jnp.int32, (node, LANES), 0)
         src0 = (b - 1) * node
         dst0 = b * node
@@ -107,21 +146,24 @@
         def _(j):
             s = src[pl.ds(j, 1), :] - src0
             d = dst[pl.ds(j, 1), :] - dst0
-            s_lo = jnp.broadcast_to((s & 255).astype(F32), (LANES, LANES))
-            s_hi = jnp.broadcast_to((s >> 8).astype(F32), (LANES, LANES))
-            d_f = jnp.broadcast_to(d.astype(F32), (LANES, LANES))
-            s_cols = mm(eye2, jnp.concatenate([s_lo, s_hi], axis=1).astype(BF16), NT)
-            d_cols = mm(eye1, d_f.astype(BF16), NT)
+            across = [
+                jnp.broadcast_to(v.astype(F32), (LANES, LANES)).astype(BF16)
+                for v in (s % node, s // node, d)
+            ]
+            cols = mm(eye, jnp.concatenate(across, axis=0), NT)
             rows = pl.ds(pl.multiple_of(j * LANES, LANES), LANES)
-            for t in range(3 * node // LANES):
-                OS[rows, t * LANES:(t + 1) * LANES] = jnp.where(
-                    s_cols == lane_i + float(t * LANES), 1.0, 0.0).astype(BF16)
+
+            def hit(a, value):
+                return jnp.where(cols[:, a * LANES:(a + 1) * LANES] == value, 1.0, 0.0).astype(BF16)
+
             for t in range(node // LANES):
-                OD[rows, t * LANES:(t + 1) * LANES] = jnp.where(
-                    d_cols == lane_i + float(t * LANES), 1.0, 0.0).astype(BF16)
+                OS[rows, t * LANES:(t + 1) * LANES] = hit(0, lane_i + float(t * LANES))
+                OD[rows, t * LANES:(t + 1) * LANES] = hit(2, lane_i + float(t * LANES))
+            for t in range(3):
+                MK[rows, t * LANES:(t + 1) * LANES] = hit(1, float(t))
             ODT[:, rows] = jnp.where(jnp.broadcast_to(d, (node, LANES)) == sub_i, 1.0, 0.0).astype(BF16)
 
-        live_bp.start()
+        begin([live_bp], [])
         XS[...] = jnp.zeros(XS.shape, BF16)
         EP[...] = jnp.zeros(EP.shape, BF16)
 
@@ -144,9 +186,7 @@
 
         for d in own:
             d.wait()
-        live_bp.wait()
-        for d in halo:
-            d.wait()
+        finish(halo_r + [live_bp], halo_l)
 
         first = b * sub - side
         lane = lax.broadcasted_iota(jnp.int32, (cin, hb), 1)
@@ -163,23 +203,33 @@
         part = remote(PO, PP, s_x.at[4], r_x.at[4], me_p)
         part.start()
         part.wait()
-        RX[1] = (PO[...] + PP[...]).astype(BF16)
-        spread = [
-            remote(RX.at[1], RX.at[0], s_r.at[0], r_r.at[0], to_right),
-            remote(RX.at[1], RX.at[2], s_r.at[1], r_r.at[1], to_left),
-        ]
-        for d in spread:
-            d.start()
-        INI[...] = mm(RX[1], EP[c]).astype(BF16)
-        DIR[...] = mm(RX[1], EN[...])
-        for d in spread:
-            d.wait()
-
+        RO[...] = (PO[...] + PP[...]).astype(BF16)
+        spread_r = [remote(RO, RN.at[:, 0:LANES], s_r.at[0], r_r.at[0], to_right)]
+        spread_l = [remote(RO, RN.at[:, LANES:2 * LANES], s_r.at[1], r_r.at[1], to_left)]
+        begin(spread_r, spread_l)
+
+        @pl.when(b == 0)
+        def _():
+            RN[:, 0:LANES] = jnp.zeros((node, LANES), BF16)
+
+        @pl.when(b == n_band - 1)
+        def _():
+            RN[:, LANES:2 * LANES] = jnp.zeros((node, LANES), BF16)
+
+        INI[...] = mm(RO[...], EP[c]).astype(BF16)
+        DIR[...] = mm(RO[...], EN[...])
         for t in range(steps):
             rows = slice(t * step_e, (t + 1) * step_e)
-            gs = mm(OS[rows, 0:node], RX[0]) + mm(OS[rows, node:2 * node], RX[1]) + mm(OS[rows, 2 * node:3 * node], RX[2])
-            gd = mm(OD[rows, :], RX[1])
-            g = jnp.concatenate([gs, gd], axis=1).astype(BF16)
+            GO[rows, 0:LANES] = mm(OS[rows, :], RO[...]).astype(BF16) * MK[rows, LANES:2 * LANES]
+            GO[rows, LANES:2 * LANES] = mm(OD[rows, :], RO[...]).astype(BF16)
+        finish(spread_r, spread_l)
+
+        for t in range(steps):
+            rows = slice(t * step_e, (t + 1) * step_e)
+            far = mm(OS[rows, :], RN[...]).astype(BF16)
+            gs = GO[rows, 0:LANES] + far[:, 0:LANES] * MK[rows, 0:LANES]
+            gs = gs + far[:, LANES:2 * LANES] * MK[rows, 2 * LANES:3 * LANES]
+            g = jnp.concatenate([gs, GO[rows, LANES:2 * LANES]], axis=1)
             u = mm(g, EW[...])
             HB[rows, :] = (u + u * jnp.tanh(u)).astype(BF16)
         SB[c] = mm(ODT[...], HB[...]).astype(BF16)
@@ -198,6 +248,9 @@
     V = pltpu.VMEM
     D = pltpu.SemaphoreType.DMA
     scratch = [
+        pltpu.SMEM((1, kblocks), jnp.int32),
+        V((edges // LANES, LANES), jnp.int32),
+        V((edges // LANES, LANES), jnp.int32),
         V((ext, cin, hb), BF16),
         V((LANES, kblocks * hb), BF16),
         V((node, kblocks * hb), BF16),
@@ -210,34 +263,36 @@
         V((2 * LANES, half), BF16),
         V((LANES, half), BF16),
         V((2, half, half), BF16),
-        V((edges, 3 * node), BF16),
+        V((edges, node), BF16),
         V((edges, node), BF16),
         V((node, edges), BF16),
+        V((edges, 3 * LANES), BF16),
         V((edges, half), BF16),
         V((8, hb), jnp.int32),
         V((8, hb), jnp.int32),
         V((node, LANES), F32),
         V((node, LANES), F32),
-        V((3, node, LANES), BF16),
-        V((8, LANES), BF16),
+        V((node, LANES), BF16),
+        V((node, 2 * LANES), BF16),
+        V((edges, 2 * LANES), BF16),
         V((node, half), F32),
         V((node, half), BF16),
         V((2, node, half), BF16),
         V((2, node, half), BF16),
         D((side,)), D((side,)), D((side,)), D((side,)),
-        D((7,)), D((7,)), D((2,)), D((2,)), D((5,)), D((sub,)), D((kblocks,)),
+        D((7,)), D((7,)), D((2,)), D((2,)), D((5,)), D((sub,)), D((kblocks,)), D((3,)),
     ]
     smem = pl.BlockSpec(memory_space=pltpu.SMEM)
     vmem = pl.BlockSpec(memory_space=pltpu.VMEM)
-    hbm = pl.BlockSpec(memory_space=pl.ANY)
+    hbm = pl.BlockSpec(memory_space=pltpu.HBM)
     return pl.pallas_call(
         kernel,
         out_shape=jax.ShapeDtypeStruct((node, half), BF16),
-        in_specs=[smem, smem, smem, vmem, vmem] + [hbm] * 7,
+        in_specs=[smem, smem] + [hbm] * 10,
         out_specs=vmem,
         scratch_shapes=scratch,
         compiler_params=pltpu.CompilerParams(
-            collective_id=0, has_side_effects=True, vmem_limit_bytes=63 * 1024 * 1024
+            collective_id=0, has_side_effects=True, vmem_limit_bytes=48 * 1024 * 1024
         ),
         name="remap_layer",
     )
@@ -253,12 +308,14 @@
         hidden = edge_in_weight.shape[1]
         edges = edge_src.shape[0]
         call = build(n_band, cin, points, kblocks, node, blk, hidden, edges)
-        return call(
-            block_ids, block_count, band_points,
+        operands = (
+            block_ids,
             edge_src.reshape(-1, LANES), edge_dst.reshape(-1, LANES),
             grid_field, block_weight, embed_weight, edge_in_weight,
             edge_out_weight, node_in_weight, node_out_weight,
         )
+        operands = [pltpu.with_memory_space_constraint(x, pltpu.HBM) for x in operands]
+        return call(block_count, band_points, *operands)
 
     return jax.shard_map(
         on_device,

time: 58.3 us -> 47.3 us (0.81)
  the two profiles are of different devices: /device:TPU:1 before, /device:TPU:129 now
where the time goes in v2:
time: 47.3 us; the launch traced here: 47.1 us
  Pallas kernels  45.1 us (95%)
  between operations  1.3 us (3%)
  local copies, waits for them, and re-layouts  0.71 us (2%)
    pallas_call x1, Pallas kernels, on_device(): return call(block_count, band_points, *operands)  45.1 us

profile of v2, /device:TPU:129, one launch (start us, length us, event | category | flops | bytes accessed | tf_op | source)
XLA Modules:
  0.0 47.1 jit_solution(60422261470938633)
XLA Ops:
  1.3 45.1 %remap_layer.1 = bf16[256,512]{1,0:T(8,128)(2,1)S(1)} custom-call(s32[1]{0:T(128)S(6)} %copy.15.cnt, s32[1]{0:T(128)S(6)} %copy.14.bp, s32[1,16]{1,0:T(1,128)} %ids_h.1, s32[40,128]{1,0:T(8,128)} %bitcast.2, s32[40,128]{1,0:T(8,128)} %bitcast.3, bf16[100,16384]{1,0:T(8,128)(2,1)} %field.1, bf16[1,16,256,512]{3,2,1,0:T(8,128)(2,1)} %bw.1, ...), custom_call_target="tpu_custom_call" | custom-call | tf_op jit(solution)/shard_map/remap_layer/pallas_call | solution.py:318
  46.4 0.7 %copy.16 = bf16[256,512]{1,0:T(8,128)(2,1)} copy(bf16[256,512]{1,0:T(8,128)(2,1)S(1)} %remap_layer.1) | data formatting | bytes 524288
